TPU v7x, 32 devices: a whole 2x2x4 slice. The times are simulated.
32 devices in a mesh: row: 8 (over z, x), col: 4 (over y, core).
Axes of the slice: x: 2, y: 2, z: 4, core: 2. Of those that a mesh axis runs over, the one named last changes fastest.
Arguments:
- field: bfloat16 [32, 1024, 2048], P(None, 'row', 'col'), may hold values from -6 to 6
- solid_flags: int32 [32, 128, 128], P(None, 'row', 'col'), may hold values 0 or 1
- deriv_matrix: bfloat16 [2048, 2048], replicated, may hold values from -0.125 to 0.125
Outputs:
- filtered: bfloat16 [32, 1024, 2048], P('col', 'row')
- deriv_z: bfloat16 [32, 1024, 2048], P('col', 'row')
Inputs may be any that keep to these rules, and one draw needn't show every extreme that they name: `solid_flags`: 1 marks a solid block, 0 a fluid one.
All inputs are finite; a program needn't handle non-finite values.
Results may differ from a plain program's by a relative error of at most 0.0058.
Values may be sent and summed in bfloat16 or wider, within the bound.
A program may use at most 128 MiB of HBM per device.

v0:
```python
import jax
import jax.numpy as jnp
from jax import lax
from jax.sharding import PartitionSpec as P

YBLK = 8
ZBLK = 16


filter_taps = ((-3, 1.0), (-2, -6.0), (-1, 15.0), (0, -20.0), (1, 15.0), (2, -6.0), (3, 1.0))


def with_halo(block, sides, width):
    for axis, dim in sides:
        count = lax.axis_size(axis)
        forward = [(i, i + 1) for i in range(count - 1)]
        forward.append((count - 1, 0))
        backward = [(target, source) for source, target in forward]
        low = lax.ppermute(
            lax.slice_in_dim(block, block.shape[dim] - width, None, axis=dim), axis, forward
        )
        high = lax.ppermute(lax.slice_in_dim(block, 0, width, axis=dim), axis, backward)
        block = jnp.concatenate([low, block, high], axis=dim)
    return block


def smooth_padded(padded, axis, length):
    center = lax.slice_in_dim(padded, 3, 3 + length, axis=axis).astype(jnp.float32)
    total = center
    for offset, tap in filter_taps:
        shifted = lax.slice_in_dim(padded, 3 + offset, 3 + offset + length, axis=axis)
        total = total + tap / 64.0 * shifted.astype(jnp.float32)
    return total


def shards(field, solid_flags, deriv_matrix):
    xcount, ycount, zcount = field.shape
    blocks = solid_flags.astype(jnp.float32)
    nyb = blocks.shape[1]
    nzb = blocks.shape[2]
    solid = jnp.broadcast_to(blocks[:, :, None, :, None], (xcount, nyb, YBLK, nzb, ZBLK)).reshape(
        xcount, ycount, zcount
    )
    masked = (field.astype(jnp.float32) * (1.0 - solid)).astype(jnp.bfloat16)
    ypadded = with_halo(masked, (("row", 1),), 3)
    yfilt = smooth_padded(ypadded, 1, ycount).astype(jnp.bfloat16)
    lines = lax.all_to_all(yfilt, "col", split_axis=0, concat_axis=2, tiled=True)
    full = lines.shape[2]
    padded = jnp.concatenate([lines[:, :, full - 3 :], lines, lines[:, :, :3]], axis=2)
    ready = smooth_padded(padded, 2, full).astype(jnp.bfloat16)
    flat = ready.reshape(-1, ready.shape[2])
    deriv = jnp.dot(flat, deriv_matrix, preferred_element_type=jnp.float32).astype(jnp.bfloat16)
    deriv_z = deriv.reshape(ready.shape)
    return (ready, deriv_z)


def solution(mesh):
    in_specs = (P(None, "row", "col"), P(None, "row", "col"), P())
    out_specs = (P("col", "row", None), P("col", "row", None))
    return jax.shard_map(shards, mesh=mesh, in_specs=in_specs, out_specs=out_specs, check_vma=False)
```

profile of v0, /device:TPU:1, one launch (start us, length us, event | category | flops | bytes accessed | tf_op | source)
XLA Modules:
  0.0 160.3 jit_solution(5055118687871779255)
XLA Ops:
  0.6 1.0 convert_subtract_fusion
  1.6 0.2 copy.45
  1.8 11.1 %broadcast_in_dim.2 = f32[32,16,8,32,16]{0,4,3,2,1:T(8,128)} broadcast(f32[32,16,32]{0,2,1:T(8,128)S(1)} %copy.45), dimensions={0,1,3} | broadcast | bytes 8454144 | tf_op jit(solution)/shard_map/broadcast_in_dim | solution.py:41
  12.9 22.3 %copy.46 = f32[32,128,512]{2,1,0:T(8,128)} copy(f32[32,128,512]{0,2,1:T(8,128)} %bitcast.9) | data formatting | bytes 16777216 | tf_op jit(solution)/shard_map/sub | solution.py:44
  35.2 6.2 %multiply_convert_fusion = bf16[32,128,512]{2,1,0:T(8,128)(2,1)S(1)} fusion(f32[32,128,512]{2,1,0:T(8,128)} %copy.46, bf16[32,128,512]{2,1,0:T(8,128)(2,1)} %param.3), kind=kLoop, calls=%fused_computation.18 | loop fusion | flops 6291456 | bytes 16777216 | tf_op jit(solution)/shard_map/convert_element_type | solution.py:44
  41.4 0.1 fusion.23
  41.5 2.1 %collective-permute-start = (bf16[32,3,512]{2,1,0:T(4,128)(2,1)S(1)}, bf16[32,3,512]{2,1,0:T(4,128)(2,1)S(1)}, u32[]{:S(2)}, u32[]{:S(2)}) collective-permute-start(bf16[32,3,512]{2,1,0:T(4,128)(2,1)S(1)} %get-tuple-element.14), channel_id=1, source_target_pairs={{0,4},{4,8},{8,12},{12,16},{16,20},{20,24},{24,28},{28,0},{1,5},{5... | collective-permute-start | bytes 294920 | tf_op jit(solution)/shard_map/ppermute | solution.py:19
  43.6 3.1 %collective-permute-start.1 = (bf16[32,3,512]{2,1,0:T(4,128)(2,1)S(1)}, bf16[32,3,512]{2,1,0:T(4,128)(2,1)S(1)}, u32[]{:S(2)}, u32[]{:S(2)}) collective-permute-start(bf16[32,3,512]{2,1,0:T(4,128)(2,1)S(1)} %get-tuple-element.15), channel_id=1, source_target_pairs={{4,0},{8,4},{12,8},{16,12},{20,16},{24,20},{28,24},{0,28},{5,1},{9... | collective-permute-start | bytes 294920 | tf_op jit(solution)/shard_map/ppermute | solution.py:22
  46.7 3.1 %collective-permute-done = bf16[32,3,512]{2,1,0:T(4,128)(2,1)S(1)} collective-permute-done((bf16[32,3,512]{2,1,0:T(4,128)(2,1)S(1)}, bf16[32,3,512]{2,1,0:T(4,128)(2,1)S(1)}, u32[]{:S(2)}, u32[]{:S(2)}) %collective-permute-start) | collective-permute-done | bytes 98336 | tf_op jit(solution)/shard_map/ppermute | solution.py:19
  49.8 0.0 collective-permute-done.1
  49.8 8.9 %fusion.6 = bf16[32,128,512]{2,1,0:T(8,128)(2,1)S(1)} fusion(bf16[32,128,512]{2,1,0:T(8,128)(2,1)S(1)} %multiply_convert_fusion, bf16[32,3,512]{2,1,0:T(4,128)(2,1)S(1)} %collective-permute-done.1, bf16[32,3,512]{2,1,0:T(4,128)(2,1)S(1)} %collective-permute-done), kind=kLoop, calls=%fused_computation.10 | loop fusion | flops 83886080 | bytes 8585216 | tf_op jit(solution)/shard_map/convert_element_type | solution.py:46
  58.8 53.0 %all_to_all.18 = bf16[32,128,512]{2,1,0:T(8,128)(2,1)} all-to-all(bf16[32,128,512]{2,1,0:T(8,128)(2,1)S(1)} %fusion.6), channel_id=1, replica_groups=mesh['row'=8,'col'=4] {'col'}, dimensions={0} | all-to-all | bytes 8388608 | tf_op jit(solution)/shard_map/all_to_all | solution.py:47
  111.8 6.4 %copy.47 = bf16[8,128,4,512]{1,3,2,0:T(8,128)(2,1)} copy(bf16[8,128,4,512]{3,1,0,2:T(8,128)(2,1)} %bitcast.12) | data formatting | bytes 8388608 | tf_op jit(solution)/shard_map/all_to_all | solution.py:47
  118.2 0.7 fusion.22
  118.9 21.2 %fusion.13 = bf16[8,128,2048]{1,2,0:T(8,128)(2,1)} fusion(bf16[8,128,2048]{1,2,0:T(8,128)(2,1)} %bitcast.11, bf16[8,128,3]{1,2,0:T(4,128)(2,1)S(1)} %get-tuple-element.13, bf16[8,128,3]{1,2,0:T(4,128)(2,1)S(1)} %get-tuple-element.12), kind=kLoop, calls=%fused_computation.17 | loop fusion | flops 83886080 | bytes 8400896 | tf_op jit(solution)/shard_map/convert_element_type | solution.py:50
  140.1 6.4 %copy.49 = bf16[8,128,2048]{2,1,0:T(8,128)(2,1)} copy(bf16[8,128,2048]{1,2,0:T(8,128)(2,1)} %fusion.13) | data formatting | bytes 8388608
  146.6 13.8 %convolution_convert_fusion = bf16[1024,2048]{1,0:T(8,128)(2,1)} fusion(bf16[1024,2048]{1,0:T(8,128)(2,1)} %bitcast.13, bf16[2048,2048]{1,0:T(8,128)(2,1)} %param.5), kind=kOutput, calls=%fused_computation.39 | convolution fusion | flops 8592031744 | bytes 16777216 | tf_op jit(solution)/shard_map/dot_general | solution.py:52
Async XLA Ops:
  41.5 8.3 %collective-permute-start = (bf16[32,3,512]{2,1,0:T(4,128)(2,1)S(1)}, bf16[32,3,512]{2,1,0:T(4,128)(2,1)S(1)}, u32[]{:S(2)}, u32[]{:S(2)}) collective-permute-start(bf16[32,3,512]{2,1,0:T(4,128)(2,1)S(1)} %get-tuple-element.14), channel_id=1, source_target_pairs={{0,4},{4,8},{8,12},{12,16},{16,20},{20,24},{24,28},{28,0},{1,5},{5... | collective-permute-start | bytes 294920 | tf_op jit(solution)/shard_map/ppermute | solution.py:19
  43.6 6.2 %collective-permute-start.1 = (bf16[32,3,512]{2,1,0:T(4,128)(2,1)S(1)}, bf16[32,3,512]{2,1,0:T(4,128)(2,1)S(1)}, u32[]{:S(2)}, u32[]{:S(2)}) collective-permute-start(bf16[32,3,512]{2,1,0:T(4,128)(2,1)S(1)} %get-tuple-element.15), channel_id=1, source_target_pairs={{4,0},{8,4},{12,8},{16,12},{20,16},{24,20},{28,24},{0,28},{5,1},{9... | collective-permute-start | bytes 294920 | tf_op jit(solution)/shard_map/ppermute | solution.py:22
where the time goes:
time: 162 us; the launch traced here: 160 us
  blocking collectives  53 us (33%)
  local copies, waits for them, and re-layouts  47.3 us (29%)
  other arithmetic  37.2 us (23%)
  matrix products  13.8 us (9%)
  starting transfers between devices  5.19 us (3%)
  waiting for transfers between devices  3.14 us (2%)
    all_to_all x1, blocking collectives, shards(): lax.all_to_all(yfilt, 'col', split_axis=0, concat_axis=2, tiled=True)  53 us
    sub x2, local copies, waits for them, and re-layouts, shards(): masked = (field.astype(jnp.float32) * (1.0 - solid)).astype(jnp.bfloat16)  22.5 us
    convert_element_type x1, other arithmetic, shards(): ready = smooth_padded(padded, 2, full).astype(jnp.bfloat16)  21.2 us
    dot_general x1, matrix products, shards(): jnp.dot(flat, deriv_matrix, preferred_element_type=jnp.float32)  13.8 us
    broadcast_in_dim x1, local copies, waits for them, and re-layouts, shards(): jnp.broadcast_to(blocks[:, :, None, :, None], (xcount, nyb, YBLK, nzb, ZB...  11.1 us
    convert_element_type x1, other arithmetic, shards(): yfilt = smooth_padded(ypadded, 1, ycount).astype(jnp.bfloat16)  8.91 us
    unnamed x1, local copies, waits for them, and re-layouts  6.43 us
    all_to_all x1, local copies, waits for them, and re-layouts, shards(): lax.all_to_all(yfilt, 'col', split_axis=0, concat_axis=2, tiled=True)  6.43 us
  transfers between devices with their start and end apart: 2, of which 1 were waited for; matrix products, arithmetic and copies ran while one was open for 0% of the time, Pallas kernels for 0%

commit v1 on v0

v1 whole, which is shorter than its diff:
```python
import functools

import jax
import jax.numpy as jnp
from jax import lax
from jax.experimental import pallas as pl
from jax.experimental.pallas import tpu as pltpu
from jax.sharding import PartitionSpec as P

MESH = pl.DeviceIdType.MESH
HALO = 16
PAD = 128
WIDE = 256
TAPS = ((-3, 1.0), (-2, -6.0), (-1, 15.0), (0, 44.0), (1, 15.0), (2, -6.0), (3, 1.0))


def band(shape, source_dim, source_shift):
    source = lax.broadcasted_iota(jnp.int32, shape, source_dim) - source_shift
    target = lax.broadcasted_iota(jnp.int32, shape, 1 - source_dim)
    offset = source - target
    taps = jnp.zeros(shape, jnp.float32)
    for at, tap in TAPS:
        taps = jnp.where(offset == at, tap / 64.0, taps)
    return taps.astype(jnp.bfloat16)


def spread(shape, block_dim, size):
    block = lax.broadcasted_iota(jnp.int32, shape, block_dim) * size
    cell = lax.broadcasted_iota(jnp.int32, shape, 1 - block_dim)
    return jnp.where((cell >= block) & (cell < block + size), 1.0, 0.0).astype(jnp.bfloat16)


def exchange(
    rows, cols, early,
    field, flags, matrix,
    filt, deriv, dense,
    raw, keep, ext, ysend, lines, wz,
    load_sem, flag_sem, matrix_sem, halo_send, halo_recv, line_send, line_recv, flag_buf,
):
    r = lax.axis_index("row")
    c = lax.axis_index("col")
    up, down = lax.rem(r + 1, rows), lax.rem(r + rows - 1, rows)
    steps, ny, full = filt.shape
    nx, _, zl = field.shape
    nyb, nzb = flags.shape[1:]
    half = cols // 2
    order = [half] + [k for k in range(1, cols) if k != half]

    def peer(k):
        return lax.rem(c + k, cols)

    def load(s, k):
        return pltpu.make_async_copy(field.at[peer(k) * steps + s], raw.at[s, k], load_sem.at[s, k])

    flag_copy = pltpu.make_async_copy(flags, flag_buf, flag_sem)
    flag_copy.start()

    def start_loads(s, carry):
        for k in range(cols):
            load(s, k).start()
        return carry

    lax.fori_loop(0, steps, start_loads, 0)
    matrix_copy = pltpu.make_async_copy(matrix, dense, matrix_sem)
    matrix_copy.start()

    barrier = pltpu.get_barrier_semaphore()
    for k in order:
        pl.semaphore_signal(barrier, inc=1, device_id=(r, peer(k)), device_id_type=MESH)
    for side in (up, down):
        pl.semaphore_signal(barrier, inc=1, device_id=(side, c), device_id_type=MESH)

    flag_copy.wait()
    fluid = (1 - flag_buf[...]).astype(jnp.float32).astype(jnp.bfloat16).reshape(nx * nyb, nzb)
    widen = spread((nzb, zl), 0, zl // nzb)
    keep[...] = (
        jnp.dot(fluid, widen, preferred_element_type=jnp.float32)
        .astype(jnp.bfloat16)
        .reshape(nx, nyb, zl)
    )
    tall = spread((ny, nyb), 1, ny // nyb)
    wy = band((ny, ny + 2 * HALO), 1, HALO)

    def mask(s):
        for k in range(cols):
            load(s, k).wait()
            cover = jnp.dot(tall, keep[peer(k) * steps + s], preferred_element_type=jnp.float32)
            ext[s, k, HALO:HALO + ny, :] = (raw[s, k].astype(jnp.float32) * cover).astype(jnp.bfloat16)

    def halos(s):
        return (
            pltpu.make_async_remote_copy(
                src_ref=ext.at[s, :, pl.ds(ny, HALO), :],
                dst_ref=ext.at[s, :, pl.ds(0, HALO), :],
                send_sem=halo_send.at[0, s], recv_sem=halo_recv.at[0, s],
                device_id=(up, c), device_id_type=MESH,
            ),
            pltpu.make_async_remote_copy(
                src_ref=ext.at[s, :, pl.ds(HALO, HALO), :],
                dst_ref=ext.at[s, :, pl.ds(ny + HALO, HALO), :],
                send_sem=halo_send.at[1, s], recv_sem=halo_recv.at[1, s],
                device_id=(down, c), device_id_type=MESH,
            ),
        )

    mine = pl.ds(pl.multiple_of(PAD + c * zl, 128), zl)

    def hand(s, k):
        return pltpu.make_async_remote_copy(
            src_ref=ysend.at[s, k],
            dst_ref=lines.at[s, :, mine],
            send_sem=line_send.at[s, k], recv_sem=line_recv.at[s, k],
            device_id=(r, peer(k)), device_id_type=MESH,
        )

    mask(0)
    pl.semaphore_wait(barrier, cols + 1)
    for copy in halos(0):
        copy.start()

    def produce(s, carry):
        @pl.when(s + 1 < steps)
        def _():
            mask(s + 1)
            for copy in halos(s + 1):
                copy.start()

        for copy in halos(s):
            copy.wait_recv()
        for k in order:
            ysend[s, k] = jnp.dot(wy, ext[s, k], preferred_element_type=jnp.float32).astype(jnp.bfloat16)
            hand(s, k).start()
        lines[s, :, mine] = jnp.dot(wy, ext[s, 0], preferred_element_type=jnp.float32).astype(jnp.bfloat16)
        return carry

    lax.fori_loop(0, steps, produce, 0)
    wz[...] = band((WIDE + 2 * PAD, WIDE), 0, PAD)
    matrix_copy.wait()

    def smooth(s):
        for k in order:
            hand(s, k).wait_recv()
        lines[s, :, 0:PAD] = lines[s, :, full:full + PAD]
        lines[s, :, full + PAD:full + 2 * PAD] = lines[s, :, PAD:2 * PAD]
        for j in range(0, full, WIDE):
            filt[s, :, j:j + WIDE] = jnp.dot(
                lines[s, :, j:j + WIDE + 2 * PAD], wz[...], preferred_element_type=jnp.float32
            ).astype(jnp.bfloat16)

    def consume(g, carry):
        smooth(2 * g)
        smooth(2 * g + 1)
        pair = filt[pl.ds(2 * g, 2)].reshape(2 * ny, full)
        for j in range(0, full, WIDE):
            deriv[pl.ds(2 * g, 2), :, j:j + WIDE] = (
                jnp.dot(pair, dense[:, j:j + WIDE], preferred_element_type=jnp.float32)
                .astype(jnp.bfloat16)
                .reshape(2, ny, WIDE)
            )
        return carry

    lax.fori_loop(0, early // 2, consume, 0)
    for s in range(early, steps):
        smooth(s)

    def drain(s, carry):
        for copy in halos(s):
            copy.wait_send()
        for k in order:
            hand(s, k).wait_send()
        return carry

    lax.fori_loop(0, steps, drain, 0)


def finish(early, filt, deriv, dense, filt_out, deriv_out, late, sems):
    steps, ny, full = filt.shape
    first = pltpu.make_async_copy(filt, filt_out, sems.at[0])
    first.start()
    second = pltpu.make_async_copy(deriv, deriv_out.at[pl.ds(0, early)], sems.at[1])
    second.start()
    count = steps - early
    rest = filt[early:steps].reshape(count * ny, full)
    thirds = []
    for j in range(0, full, WIDE):
        late[:, :, j:j + WIDE] = (
            jnp.dot(rest, dense[:, j:j + WIDE], preferred_element_type=jnp.float32)
            .astype(jnp.bfloat16)
            .reshape(count, ny, WIDE)
        )
        copy = pltpu.make_async_copy(
            late.at[:, :, pl.ds(j, WIDE)],
            deriv_out.at[pl.ds(early, count), :, pl.ds(j, WIDE)],
            sems.at[2 + j // WIDE],
        )
        copy.start()
        thirds.append(copy)
    first.wait()
    second.wait()
    for copy in thirds:
        copy.wait()


def shards(rows, cols, field, solid_flags, deriv_matrix):
    nx, ny, zl = field.shape
    full = deriv_matrix.shape[0]
    steps = nx // cols
    early = (steps - 1) // 2 * 2
    bf16 = jnp.bfloat16
    dma = pltpu.SemaphoreType.DMA
    hbm = pl.BlockSpec(memory_space=pl.ANY)
    vmem = pl.BlockSpec(memory_space=pltpu.VMEM)
    filt, deriv, dense = pl.pallas_call(
        functools.partial(exchange, rows, cols, early),
        out_shape=(
            pltpu.VMEM((steps, ny, full), bf16),
            pltpu.VMEM((early, ny, full), bf16),
            pltpu.VMEM((full, full), bf16),
        ),
        in_specs=[hbm] * 3,
        out_specs=(vmem,) * 3,
        scratch_shapes=[
            pltpu.VMEM((steps, cols, ny, zl), bf16),
            pltpu.VMEM((nx, solid_flags.shape[1], zl), bf16),
            pltpu.VMEM((steps, cols, ny + 2 * HALO, zl), bf16),
            pltpu.VMEM((steps, cols, ny, zl), bf16),
            pltpu.VMEM((steps, ny, full + 2 * PAD), bf16),
            pltpu.VMEM((WIDE + 2 * PAD, WIDE), bf16),
            dma((steps, cols)),
            dma,
            dma,
            dma((2, steps)),
            dma((2, steps)),
            dma((steps, cols)),
            dma((steps, cols)),
            pltpu.VMEM(solid_flags.shape, jnp.int32),
        ],
        compiler_params=pltpu.CompilerParams(
            collective_id=0, has_side_effects=True, vmem_limit_bytes=36 * 1024 * 1024
        ),
        name="exchange",
    )(field, solid_flags, deriv_matrix)
    return pl.pallas_call(
        functools.partial(finish, early),
        out_shape=(
            jax.ShapeDtypeStruct((steps, ny, full), bf16),
            jax.ShapeDtypeStruct((steps, ny, full), bf16),
        ),
        in_specs=[vmem] * 3,
        out_specs=(hbm, hbm),
        scratch_shapes=[
            pltpu.VMEM((steps - early, ny, full), bf16),
            dma((2 + full // WIDE,)),
        ],
        compiler_params=pltpu.CompilerParams(vmem_limit_bytes=8 * 1024 * 1024),
        name="finish",
    )(filt, deriv, dense)


def solution(mesh):
    in_specs = (P(None, "row", "col"), P(None, "row", "col"), P())
    out_specs = (P("col", "row", None), P("col", "row", None))
    rows, cols = mesh.shape["row"], mesh.shape["col"]
    return jax.shard_map(
        functools.partial(shards, rows, cols), mesh=mesh, in_specs=in_specs, out_specs=out_specs, check_vma=False
    )
```

time: 162 us -> 62.4 us (0.39)
  Pallas kernels: 0 us -> 60.6 us
  blocking collectives: 53 us -> 0 us
  local copies, waits for them, and re-layouts: 47.3 us -> 0.94 us
  other arithmetic: 37.2 us -> 0 us
  matrix products: 13.8 us -> 0 us
  starting transfers between devices: 5.19 us -> 0 us
  waiting for transfers between devices: 3.14 us -> 0 us
    pallas_call x0 -> x2, Pallas kernels: none -> 60.6 us  [the longest x1 57.3 us: shards(): pl.pallas_call(functools.partial(exchange, rows, cols, early), out_shape=...]
    all_to_all x1 -> x0, blocking collectives: 53 us -> none  [shards(): lax.all_to_all(yfilt, 'col', split_axis=0, concat_axis=2, tiled=True)]
    convert_element_type x3 -> x0, other arithmetic: 36.3 us -> none  [the longest x1 21.2 us: shards(): ready = smooth_padded(padded, 2, full).astype(jnp.bfloat16)]
    sub x2 -> x0, local copies, waits for them, and re-layouts: 22.5 us -> none  [shards(): masked = (field.astype(jnp.float32) * (1.0 - solid)).astype(jnp.bfloat16)]
    dot_general x1 -> x0, matrix products: 13.8 us -> none  [shards(): jnp.dot(flat, deriv_matrix, preferred_element_type=jnp.float32)]
    broadcast_in_dim x1 -> x0, local copies, waits for them, and re-layouts: 11.1 us -> none  [shards(): jnp.broadcast_to(blocks[:, :, None, :, None], (xcount, nyb, YBLK, nzb, ZB...]
    all_to_all x1 -> x0, local copies, waits for them, and re-layouts: 6.43 us -> none  [shards(): lax.all_to_all(yfilt, 'col', split_axis=0, concat_axis=2, tiled=True)]
    unnamed x1 -> x2, local copies, waits for them, and re-layouts: 6.43 us -> 0.94 us
  transfers between devices with their start and end apart: 2 -> 0, of which waited for: 1 -> 0; matrix products, arithmetic and copies ran while one was open for 0% -> 0% of each run, Pallas kernels for 0% -> 0%
where the time goes in v1:
time: 62.4 us; the launch traced here: 62.2 us
  Pallas kernels  60.6 us (97%)
  local copies, waits for them, and re-layouts  0.94 us (2%)
  between operations  0.65 us (1%)
    pallas_call x1, Pallas kernels, shards(): pl.pallas_call(functools.partial(exchange, rows, cols, early), out_shape=...  57.3 us
    pallas_call x1, Pallas kernels, shards(): pl.pallas_call(functools.partial(finish, early), out_shape=(jax.ShapeDtyp...  3.35 us

profile of v1, /device:TPU:1, one launch (start us, length us, event | category | flops | bytes accessed | tf_op | source)
XLA Modules:
  0.0 62.2 jit_solution(9576262547921539865)
XLA Ops:
  0.6 0.0 copy-start
  0.6 0.9 %copy-done = s32[32,16,32]{2,1,0:T(8,128)S(1)} copy-done((s32[32,16,32]{2,1,0:T(8,128)S(1)}, s32[32,16,32]{2,1,0:T(8,128)}, u32[]{:S(2)}) %copy-start) | copy-done | bytes 65560
  1.6 57.3 %exchange.1 = (bf16[8,128,2048]{2,1,0:T(8,128)(2,1)S(1)}, bf16[6,128,2048]{2,1,0:T(8,128)(2,1)S(1)}, bf16[2048,2048]{1,0:T(8,128)(2,1)S(1)}) custom-call(bf16[32,128,512]{2,1,0:T(8,128)(2,1)} %field.1, s32[32,16,32]{2,1,0:T(8,128)S(1)} %copy-done, bf16[2048,2048]{1,0:T(8,128)(2,1)} %matrix.1), custom_call_target="tpu_custom_call" | custom-call | tf_op jit(solution)/shard_map/exchange/pallas_call | solution.py:213
  58.9 3.3 %finish.1 = (bf16[8,128,2048]{2,1,0:T(8,128)(2,1)}, bf16[8,128,2048]{2,1,0:T(8,128)(2,1)}) custom-call(bf16[8,128,2048]{2,1,0:T(8,128)(2,1)S(1)} %get-tuple-element.5.filt, bf16[6,128,2048]{2,1,0:T(8,128)(2,1)S(1)} %get-tuple-element.6.deriv, bf16[2048,2048]{1,0:T(8,128)(2,1)S(1)} %get-tuple-element.7.dense), custom_call_target="tpu_custom_call" | custom-call | tf_op jit(solution)/shard_map/finish/pallas_call | solution.py:243
Async XLA Ops:
  0.6 1.0 %copy-start = (s32[32,16,32]{2,1,0:T(8,128)S(1)}, s32[32,16,32]{2,1,0:T(8,128)}, u32[]{:S(2)}) copy-start(s32[32,16,32]{2,1,0:T(8,128)} %flags.1) | copy-start | bytes 196612

commit v2 on v1

v2 whole, which is shorter than its diff:
```python
import functools

import jax
import jax.numpy as jnp
from jax import lax
from jax.experimental import pallas as pl
from jax.experimental.pallas import tpu as pltpu
from jax.sharding import PartitionSpec as P

MESH = pl.DeviceIdType.MESH
HALO = 16
PAD = 128
WIDE = 256
TAPS = ((-3, 1.0), (-2, -6.0), (-1, 15.0), (0, 44.0), (1, 15.0), (2, -6.0), (3, 1.0))


def band(shape, source_dim, source_shift):
    source = lax.broadcasted_iota(jnp.int32, shape, source_dim) - source_shift
    target = lax.broadcasted_iota(jnp.int32, shape, 1 - source_dim)
    offset = source - target
    taps = jnp.zeros(shape, jnp.float32)
    for at, tap in TAPS:
        taps = jnp.where(offset == at, tap / 64.0, taps)
    return taps.astype(jnp.bfloat16)


def spread(shape, block_dim, size):
    block = lax.broadcasted_iota(jnp.int32, shape, block_dim) * size
    cell = lax.broadcasted_iota(jnp.int32, shape, 1 - block_dim)
    return jnp.where((cell >= block) & (cell < block + size), 1.0, 0.0).astype(jnp.bfloat16)


def exchange(
    rows, cols, early,
    field, flags, matrix,
    filt, deriv, dense, lines, wz,
    raw, keep, ext, ysend,
    load_sem, flag_sem, matrix_sem, halo_send, halo_recv, line_send, line_recv,
    part_send, part_recv, flag_buf,
):
    r = lax.axis_index("row")
    c = lax.axis_index("col")
    up, down = lax.rem(r + 1, rows), lax.rem(r + rows - 1, rows)
    ny, full = filt.shape[1:]
    nx, _, zl = field.shape
    steps = nx // cols
    nyb, nzb = flags.shape[1:]
    half = cols // 2
    order = [half] + [k for k in range(1, cols) if k != half]

    def peer(k):
        return lax.rem(c + k, cols)

    def load(s, k):
        return pltpu.make_async_copy(field.at[peer(k) * steps + s], raw.at[s, k], load_sem.at[s, k])

    def start_loads(s, carry):
        for k in order + [0]:
            load(s, k).start()
        return carry

    barrier = pltpu.get_barrier_semaphore()
    for k in order:
        pl.semaphore_signal(barrier, inc=1, device_id=(r, peer(k)), device_id_type=MESH)
    for side in (up, down):
        pl.semaphore_signal(barrier, inc=1, device_id=(side, c), device_id_type=MESH)
    flag_copy = pltpu.make_async_copy(flags, flag_buf, flag_sem)
    flag_copy.start()
    lax.fori_loop(0, steps, start_loads, 0)
    matrix_copy = pltpu.make_async_copy(matrix, dense, matrix_sem)
    matrix_copy.start()

    flag_copy.wait()
    fluid = (1 - flag_buf[...]).astype(jnp.float32).astype(jnp.bfloat16).reshape(nx * nyb, nzb)
    widen = spread((nzb, zl), 0, zl // nzb)
    keep[...] = (
        jnp.dot(fluid, widen, preferred_element_type=jnp.float32)
        .astype(jnp.bfloat16)
        .reshape(nx, nyb, zl)
    )
    tall = spread((ny, nyb), 1, ny // nyb)
    inner = ny - 2 * HALO
    wy = band((ny, ny + 2 * HALO), 1, HALO)
    winner = band((inner, ny), 1, HALO)
    wedge = band((HALO, 3 * HALO), 1, HALO)
    cuts = (pl.ds(HALO, inner), pl.ds(0, HALO), pl.ds(ny - HALO, HALO))

    def mask(s):
        for k in order + [0]:
            load(s, k).wait()
            cover = jnp.dot(tall, keep[peer(k) * steps + s], preferred_element_type=jnp.float32)
            ext[s, k, HALO:HALO + ny, :] = (raw[s, k].astype(jnp.float32) * cover).astype(jnp.bfloat16)

    def halos(s):
        return (
            pltpu.make_async_remote_copy(
                src_ref=ext.at[s, :, pl.ds(ny, HALO), :],
                dst_ref=ext.at[s, :, pl.ds(0, HALO), :],
                send_sem=halo_send.at[0, s], recv_sem=halo_recv.at[0, s],
                device_id=(up, c), device_id_type=MESH,
            ),
            pltpu.make_async_remote_copy(
                src_ref=ext.at[s, :, pl.ds(HALO, HALO), :],
                dst_ref=ext.at[s, :, pl.ds(ny + HALO, HALO), :],
                send_sem=halo_send.at[1, s], recv_sem=halo_recv.at[1, s],
                device_id=(down, c), device_id_type=MESH,
            ),
        )

    mine = pl.ds(pl.multiple_of(PAD + c * zl, 128), zl)

    def hand(s, k):
        return pltpu.make_async_remote_copy(
            src_ref=ysend.at[s, k],
            dst_ref=lines.at[s, :, mine],
            send_sem=line_send.at[s, k], recv_sem=line_recv.at[s, k],
            device_id=(r, peer(k)), device_id_type=MESH,
        )

    def part(k, p):
        return pltpu.make_async_remote_copy(
            src_ref=ysend.at[0, k, cuts[p]],
            dst_ref=lines.at[0, cuts[p], mine],
            send_sem=part_send.at[p, k], recv_sem=part_recv.at[p, k],
            device_id=(r, peer(k)), device_id_type=MESH,
        )

    def apply(weights, block):
        return jnp.dot(weights, block, preferred_element_type=jnp.float32).astype(jnp.bfloat16)

    mask(0)
    pl.semaphore_wait(barrier, cols + 1)
    for copy in halos(0):
        copy.start()
    for k in order:
        ysend[0, k, HALO:HALO + inner] = apply(winner, ext[0, k, HALO:HALO + ny])
        part(k, 0).start()

    def advance(s):
        @pl.when(s + 1 < steps)
        def _():
            mask(s + 1)
            for copy in halos(s + 1):
                copy.start()

        for copy in halos(s):
            copy.wait_recv()

    advance(0)
    for k in order:
        ysend[0, k, 0:HALO] = apply(wedge, ext[0, k, 0:3 * HALO])
        part(k, 1).start()
        ysend[0, k, ny - HALO:ny] = apply(wedge, ext[0, k, ny - HALO:ny + 2 * HALO])
        part(k, 2).start()
    lines[0, :, mine] = apply(wy, ext[0, 0])

    def produce(s, carry):
        advance(s)
        for k in order:
            ysend[s, k] = apply(wy, ext[s, k])
            hand(s, k).start()
        lines[s, :, mine] = apply(wy, ext[s, 0])
        return carry

    lax.fori_loop(1, steps, produce, 0)
    wz[...] = band((WIDE + 2 * PAD, WIDE), 0, PAD)
    matrix_copy.wait()

    def arrive(s):
        for k in order:
            hand(s, k).wait_recv()

    def smooth(s):
        smooth_line(lines.at[s], wz, filt.at[s])

    def multiply(s, count):
        block = filt[pl.ds(s, count)].reshape(count * ny, full)
        for j in range(0, full, WIDE):
            deriv[pl.ds(s, count), :, j:j + WIDE] = apply(block, dense[:, j:j + WIDE]).reshape(count, ny, WIDE)

    def consume(g, carry):
        for s in (2 * g, 2 * g + 1):
            arrive(s)
            smooth(s)
        multiply(2 * g, 2)
        return carry

    for k in order:
        for p in range(3):
            part(k, p).wait_recv()
    smooth(0)
    arrive(1)
    smooth(1)
    multiply(0, 2)
    lax.fori_loop(1, early // 2, consume, 0)
    if early % 2:
        arrive(early - 1)
        smooth(early - 1)
        multiply(early - 1, 1)
    for copy in halos(0):
        copy.wait_send()
    for k in order:
        for p in range(3):
            part(k, p).wait_send()

    def drain(s, carry):
        for copy in halos(s):
            copy.wait_send()
        for k in order:
            hand(s, k).wait_send()
        return carry

    lax.fori_loop(1, steps, drain, 0)
    for s in range(early, steps):
        arrive(s)


def smooth_line(line, wz, out):
    full = out.shape[1]
    line[:, 0:PAD] = line[:, full:full + PAD]
    line[:, full + PAD:full + 2 * PAD] = line[:, PAD:2 * PAD]
    for j in range(0, full, WIDE):
        out[:, j:j + WIDE] = jnp.dot(
            line[:, j:j + WIDE + 2 * PAD], wz[...], preferred_element_type=jnp.float32
        ).astype(jnp.bfloat16)


def finish(filt, deriv, dense, lines, wz, filt_out, deriv_out, line, last, late, sems):
    early, ny, full = filt.shape
    copies = [
        pltpu.make_async_copy(filt, filt_out.at[pl.ds(0, early)], sems.at[0]),
        pltpu.make_async_copy(deriv, deriv_out.at[pl.ds(0, early)], sems.at[1]),
    ]
    for copy in copies:
        copy.start()
    line[...] = lines[early]
    smooth_line(line, wz, last)
    copies.append(pltpu.make_async_copy(last, filt_out.at[early], sems.at[2]))
    copies[-1].start()
    for j in range(0, full, WIDE):
        late[:, j:j + WIDE] = jnp.dot(
            last[...], dense[:, j:j + WIDE], preferred_element_type=jnp.float32
        ).astype(jnp.bfloat16)
        copies.append(
            pltpu.make_async_copy(
                late.at[:, pl.ds(j, WIDE)], deriv_out.at[early, :, pl.ds(j, WIDE)], sems.at[3 + j // WIDE]
            )
        )
        copies[-1].start()
    for copy in copies:
        copy.wait()


def shards(rows, cols, field, solid_flags, deriv_matrix):
    nx, ny, zl = field.shape
    full = deriv_matrix.shape[0]
    steps = nx // cols
    early = steps - 1
    bf16 = jnp.bfloat16
    dma = pltpu.SemaphoreType.DMA
    hbm = pl.BlockSpec(memory_space=pl.ANY)
    vmem = pl.BlockSpec(memory_space=pltpu.VMEM)
    held = pl.pallas_call(
        functools.partial(exchange, rows, cols, early),
        out_shape=(
            pltpu.VMEM((early, ny, full), bf16),
            pltpu.VMEM((early, ny, full), bf16),
            pltpu.VMEM((full, full), bf16),
            pltpu.VMEM((steps, ny, full + 2 * PAD), bf16),
            pltpu.VMEM((WIDE + 2 * PAD, WIDE), bf16),
        ),
        in_specs=[hbm] * 3,
        out_specs=(vmem,) * 5,
        scratch_shapes=[
            pltpu.VMEM((steps, cols, ny, zl), bf16),
            pltpu.VMEM((nx, solid_flags.shape[1], zl), bf16),
            pltpu.VMEM((steps, cols, ny + 2 * HALO, zl), bf16),
            pltpu.VMEM((steps, cols, ny, zl), bf16),
            dma((steps, cols)),
            dma,
            dma,
            dma((2, steps)),
            dma((2, steps)),
            dma((steps, cols)),
            dma((steps, cols)),
            dma((3, cols)),
            dma((3, cols)),
            pltpu.VMEM(solid_flags.shape, jnp.int32),
        ],
        compiler_params=pltpu.CompilerParams(
            collective_id=0, has_side_effects=True, vmem_limit_bytes=43 * 1024 * 1024
        ),
        name="exchange",
    )(field, solid_flags, deriv_matrix)
    return pl.pallas_call(
        finish,
        out_shape=(
            jax.ShapeDtypeStruct((steps, ny, full), bf16),
            jax.ShapeDtypeStruct((steps, ny, full), bf16),
        ),
        in_specs=[vmem] * 5,
        out_specs=(hbm, hbm),
        scratch_shapes=[
            pltpu.VMEM((ny, full + 2 * PAD), bf16),
            pltpu.VMEM((ny, full), bf16),
            pltpu.VMEM((ny, full), bf16),
            dma((3 + full // WIDE,)),
        ],
        compiler_params=pltpu.CompilerParams(vmem_limit_bytes=8 * 1024 * 1024),
        name="finish",
    )(*held)


def solution(mesh):
    in_specs = (P(None, "row", "col"), P(None, "row", "col"), P())
    out_specs = (P("col", "row", None), P("col", "row", None))
    rows, cols = mesh.shape["row"], mesh.shape["col"]
    return jax.shard_map(
        functools.partial(shards, rows, cols), mesh=mesh, in_specs=in_specs, out_specs=out_specs, check_vma=False
    )
```

time: 62.4 us -> 58.8 us (0.942)
  Pallas kernels: 60.6 us -> 58 us
  local copies, waits for them, and re-layouts: 0.94 us -> 0 us
    pallas_call x1, Pallas kernels: 57.3 us -> 54.6 us  [shards(): pl.pallas_call(functools.partial(exchange, rows, cols, early), out_shape=...]
    unnamed x2 -> x0, local copies, waits for them, and re-layouts: 0.94 us -> none
where the time goes in v2:
time: 58.8 us; the launch traced here: 58.7 us
  Pallas kernels  58 us (99%)
  between operations  0.64 us (1%)
    pallas_call x1, Pallas kernels, shards(): pl.pallas_call(functools.partial(exchange, rows, cols, early), out_shape=...  54.6 us
    pallas_call x1, Pallas kernels, shards(): pl.pallas_call(finish, out_shape=(jax.ShapeDtypeStruct((steps, ny, full),...  3.44 us

profile of v2, /device:TPU:1, one launch (start us, length us, event | category | flops | bytes accessed | tf_op | source)
XLA Modules:
  0.0 58.7 jit_solution(143710762283537431)
XLA Ops:
  0.6 54.6 %exchange.1 = (bf16[7,128,2048]{2,1,0:T(8,128)(2,1)S(1)}, bf16[7,128,2048]{2,1,0:T(8,128)(2,1)S(1)}, bf16[2048,2048]{1,0:T(8,128)(2,1)S(1)}, bf16[8,128,2304]{2,1,0:T(8,128)(2,1)S(1)}, bf16[512,256]{1,0:T(8,128)(2,1)S(1)}) custom-call(bf16[32,128,512]{2,1,0:T(8,128)(2,1)} %field.1, s32[32,16,32]{2,1,0:T(8,128)} %flags.1, bf16[2048,2048]{1,0:T(8,128)(2,1)} %matrix.1), custom_call_target="tpu_custom_call" | custom-call | tf_op jit(solution)/shard_map/exchange/pallas_call | solution.py:263
  55.2 3.4 %finish.1 = (bf16[8,128,2048]{2,1,0:T(8,128)(2,1)}, bf16[8,128,2048]{2,1,0:T(8,128)(2,1)}) custom-call(bf16[7,128,2048]{2,1,0:T(8,128)(2,1)S(1)} %get-tuple-element.7.filt, bf16[7,128,2048]{2,1,0:T(8,128)(2,1)S(1)} %get-tuple-element.8.deriv, bf16[2048,2048]{1,0:T(8,128)(2,1)S(1)} %get-tuple-element.9.dense, ...), custom_call_target="tpu_custom_call" | custom-call | tf_op jit(solution)/shard_map/finish/pallas_call | solution.py:295

commit v3 on v2

--- a/solution.py
+++ b/solution.py
@@ -66,9 +66,8 @@
         pl.semaphore_signal(barrier, inc=1, device_id=(side, c), device_id_type=MESH)
     flag_copy = pltpu.make_async_copy(flags, flag_buf, flag_sem)
     flag_copy.start()
-    lax.fori_loop(0, steps, start_loads, 0)
+    start_loads(0, 0)
     matrix_copy = pltpu.make_async_copy(matrix, dense, matrix_sem)
-    matrix_copy.start()
 
     flag_copy.wait()
     fluid = (1 - flag_buf[...]).astype(jnp.float32).astype(jnp.bfloat16).reshape(nx * nyb, nzb)
@@ -85,11 +84,14 @@
     wedge = band((HALO, 3 * HALO), 1, HALO)
     cuts = (pl.ds(HALO, inner), pl.ds(0, HALO), pl.ds(ny - HALO, HALO))
 
+    def mask_line(s, k):
+        load(s, k).wait()
+        cover = jnp.dot(tall, keep[peer(k) * steps + s], preferred_element_type=jnp.float32)
+        ext[s, k, HALO:HALO + ny, :] = (raw[s, k].astype(jnp.float32) * cover).astype(jnp.bfloat16)
+
     def mask(s):
         for k in order + [0]:
-            load(s, k).wait()
-            cover = jnp.dot(tall, keep[peer(k) * steps + s], preferred_element_type=jnp.float32)
-            ext[s, k, HALO:HALO + ny, :] = (raw[s, k].astype(jnp.float32) * cover).astype(jnp.bfloat16)
+            mask_line(s, k)
 
     def halos(s):
         return (
@@ -128,13 +130,17 @@
     def apply(weights, block):
         return jnp.dot(weights, block, preferred_element_type=jnp.float32).astype(jnp.bfloat16)
 
-    mask(0)
-    pl.semaphore_wait(barrier, cols + 1)
+    for i, k in enumerate(order):
+        mask_line(0, k)
+        ysend[0, k, HALO:HALO + inner] = apply(winner, ext[0, k, HALO:HALO + ny])
+        if i == 0:
+            pl.semaphore_wait(barrier, cols + 1)
+        part(k, 0).start()
+    mask_line(0, 0)
     for copy in halos(0):
         copy.start()
-    for k in order:
-        ysend[0, k, HALO:HALO + inner] = apply(winner, ext[0, k, HALO:HALO + ny])
-        part(k, 0).start()
+    lax.fori_loop(1, steps, start_loads, 0)
+    matrix_copy.start()
 
     def advance(s):
         @pl.when(s + 1 < steps)

time: 58.8 us -> 59 us (level)
  no operation moved by 1% of the time
where the time goes in v3:
time: 59 us; the launch traced here: 58.9 us
  Pallas kernels  58.2 us (99%)
  between operations  0.64 us (1%)
    pallas_call x1, Pallas kernels, shards(): pl.pallas_call(functools.partial(exchange, rows, cols, early), out_shape=...  54.8 us
    pallas_call x1, Pallas kernels, shards(): pl.pallas_call(finish, out_shape=(jax.ShapeDtypeStruct((steps, ny, full),...  3.44 us

profile of v3, /device:TPU:1, one launch (start us, length us, event | category | flops | bytes accessed | tf_op | source)
XLA Modules:
  0.0 58.9 jit_solution(3763194881035327214)
XLA Ops:
  0.6 54.8 %exchange.1 = (bf16[7,128,2048]{2,1,0:T(8,128)(2,1)S(1)}, bf16[7,128,2048]{2,1,0:T(8,128)(2,1)S(1)}, bf16[2048,2048]{1,0:T(8,128)(2,1)S(1)}, bf16[8,128,2304]{2,1,0:T(8,128)(2,1)S(1)}, bf16[512,256]{1,0:T(8,128)(2,1)S(1)}) custom-call(bf16[32,128,512]{2,1,0:T(8,128)(2,1)} %field.1, s32[32,16,32]{2,1,0:T(8,128)} %flags.1, bf16[2048,2048]{1,0:T(8,128)(2,1)} %matrix.1), custom_call_target="tpu_custom_call" | custom-call | tf_op jit(solution)/shard_map/exchange/pallas_call | solution.py:269
  55.4 3.4 %finish.1 = (bf16[8,128,2048]{2,1,0:T(8,128)(2,1)}, bf16[8,128,2048]{2,1,0:T(8,128)(2,1)}) custom-call(bf16[7,128,2048]{2,1,0:T(8,128)(2,1)S(1)} %get-tuple-element.7.filt, bf16[7,128,2048]{2,1,0:T(8,128)(2,1)S(1)} %get-tuple-element.8.deriv, bf16[2048,2048]{1,0:T(8,128)(2,1)S(1)} %get-tuple-element.9.dense, ...), custom_call_target="tpu_custom_call" | custom-call | tf_op jit(solution)/shard_map/finish/pallas_call | solution.py:301
